TPU v7x, 32 devices: a whole 2x2x4 slice. The times are simulated.
32 devices in a mesh: gx: 8 (over y, x, core), gy: 4 (over z).
Axes of the slice: x: 2, y: 2, z: 4, core: 2. Of those that a mesh axis runs over, the one named last changes fastest.
Arguments:
- snapshots: bfloat16 [2, 1, 256, 256, 512], P(None, None, 'gx', 'gy'), may hold values from -12 to 12
- start: float32 [1, 32, 256, 256], P(None, None, 'gx', 'gy'), may hold values from -6 to 6
Outputs:
- basis_field: float32 [1, 32, 256, 256], P(None, None, 'gx', 'gy')
- phi: float32 [1, 2, 32, 32], replicated
All inputs are finite; a program needn't handle non-finite values.
Results may differ from a plain program's by a relative error of at most 0.0005.
Values may be sent and summed in bfloat16 or wider, within the bound.
A program may use at most 64 MiB of HBM per device.

v0:
```python
import jax
import jax.numpy as jnp
from jax import lax
from jax.sharding import PartitionSpec as P

ITERS = 4
precise = lax.Precision.HIGHEST


def swapped(x, axis, apart):
    return lax.ppermute(x, axis, [(i, i ^ 1 << apart) for i in range(lax.axis_size(axis))])


def passed_along(block, axis, distance):
    devices = range(lax.axis_size(axis))
    route = [(i - distance, i) for i in devices if i - distance in devices]
    return lax.ppermute(block, axis, route)


def inverse_factor(matrix):
    factor = jnp.linalg.cholesky(matrix)
    identity = jnp.broadcast_to(jnp.eye(matrix.shape[-1], dtype=matrix.dtype), matrix.shape)
    inverse = lax.linalg.triangular_solve(factor, identity, left_side=True, lower=True)
    return (factor, inverse)


def apply_inverse(inverse, right_side):
    return jnp.einsum("...kj,...jm->...km", inverse, right_side, precision=precise)


def shift_solve(inverse, right_matrix):
    inner = apply_inverse(inverse, right_matrix)
    return apply_inverse(jnp.swapaxes(inverse, -1, -2), inner)


def project(local_side):
    return lax.psum(local_side, ("gx", "gy"))


def gram_of(grown):
    return jnp.einsum("fkm,fjm->fkj", grown, grown, precision=precise)


def pair_grams(plus_terms, minus_terms):
    left_matrix = jnp.einsum("fkab,fjab->fkj", plus_terms, plus_terms, precision=precise)
    right_matrix = jnp.einsum("fkab,fjab->fkj", plus_terms, minus_terms, precision=precise)
    return (left_matrix, right_matrix)


def mirror_fields(stacked, rows, cols):
    moved = stacked
    for bit_number in range(lax.axis_size("gx").bit_length() - 1):
        moved = swapped(moved, "gx", bit_number)
    for bit_number in range(lax.axis_size("gy").bit_length() - 1):
        moved = swapped(moved, "gy", bit_number)
    lead = moved.shape[:-1]
    turned = moved.reshape(lead + (rows, cols))[..., ::-1, ::-1]
    return turned.reshape(moved.shape)


def shift_terms(field):
    rows = field.shape[2]
    cols = field.shape[3]
    below = passed_along(field[:, :, :1, :], "gx", -1)
    beside = passed_along(field[:, :, :, :1], "gy", -1)
    last_row_device = lax.axis_index("gx") == lax.axis_size("gx") - 1
    last_col_device = lax.axis_index("gy") == lax.axis_size("gy") - 1
    row_weight = jnp.where((jnp.arange(rows) == rows - 1) & last_row_device, 0.0, 1.0).astype(
        jnp.float32
    )
    col_weight = jnp.where((jnp.arange(cols) == cols - 1) & last_col_device, 0.0, 1.0).astype(
        jnp.float32
    )
    row_extended = jnp.concatenate([field, below], axis=2)
    col_extended = jnp.concatenate([field, beside], axis=3)
    row_plus = (row_extended[:, :, 1:] + row_extended[:, :, :-1]) * row_weight[:, None]
    row_minus = row_extended[:, :, 1:] - row_extended[:, :, :-1]
    col_plus = (col_extended[:, :, :, 1:] + col_extended[:, :, :, :-1]) * col_weight
    col_minus = col_extended[:, :, :, 1:] - col_extended[:, :, :, :-1]
    row_lhs, row_rhs = pair_grams(row_plus, row_minus)
    col_lhs, col_rhs = pair_grams(col_plus, col_minus)
    return (row_lhs, row_rhs, col_lhs, col_rhs)


def body(snapshots, start):
    frames, basis_count, rows, cols = start.shape
    upper_half = lax.axis_index("gx") < lax.axis_size("gx") // 2
    start_flat = start.reshape(frames, basis_count, rows * cols)
    own = snapshots.astype(jnp.float32).reshape(2, frames, rows * cols, -1)

    def local_side(weights, weights_mirror):
        p_real = jnp.einsum("fkm,fms->fks", weights, own[0], precision=precise)
        p_imag = jnp.einsum("fkm,fms->fks", weights, own[1], precision=precise)
        q_real = jnp.einsum("fkm,fms->fks", weights_mirror, own[0], precision=precise)
        q_imag = jnp.einsum("fkm,fms->fks", weights_mirror, own[1], precision=precise)
        first = jnp.where(upper_half, p_real - q_imag, p_imag + q_real)
        second = jnp.where(upper_half, -p_imag - q_real, p_real - q_imag)
        return jnp.concatenate([first, second], axis=-1)

    start_mirror = mirror_fields(start_flat[None], rows, cols)[0]
    basis = start_flat
    basis_mirror = start_mirror
    for step_index in range(ITERS):
        side = project(local_side(basis, basis_mirror))
        half = side.shape[-1] // 2
        side_first = side[..., :half]
        side_second = side[..., half:]
        g_real = jnp.einsum("fks,fms->fkm", side_first, own[0], precision=precise) - jnp.einsum(
            "fks,fms->fkm", side_second, own[1], precision=precise
        )
        g_imag = jnp.einsum("fks,fms->fkm", side_first, own[1], precision=precise) + jnp.einsum(
            "fks,fms->fkm", side_second, own[0], precision=precise
        )
        moved = mirror_fields(jnp.stack([g_real, g_imag]), rows, cols)
        grown = jnp.where(upper_half, g_real + moved[0], g_imag - moved[1])
        grown_mirror = jnp.where(upper_half, moved[1] - g_imag, moved[0] + g_real)
        grown, grown_mirror = (grown, grown_mirror)
        gram = lax.psum(gram_of(grown), ("gx", "gy"))
        factor, inverse = inverse_factor(gram)
        basis = apply_inverse(inverse, grown)
        basis_mirror = apply_inverse(inverse, grown_mirror)
    field = basis.reshape(frames, basis_count, rows, cols)
    local_terms = shift_terms(field)
    row_lhs, row_rhs, col_lhs, col_rhs = lax.psum(
        (local_terms[0], local_terms[1], local_terms[2], local_terms[3]), ("gx", "gy")
    )
    factors, inverses = inverse_factor(jnp.stack([row_lhs, col_lhs]))
    phi = jnp.swapaxes(shift_solve(inverses, jnp.stack([row_rhs, col_rhs])), 0, 1)
    return (field, phi)


def solution(mesh):
    return jax.shard_map(
        body,
        mesh=mesh,
        in_specs=(P(None, None, "gx", "gy", None), P(None, None, "gx", "gy")),
        out_specs=(P(None, None, "gx", "gy"), P()),
        check_vma=False,
    )
```

profile of v0, /device:TPU:0, one launch (start us, length us, event | category | flops | bytes accessed | tf_op | source)
XLA Modules:
  0.0 1151.4 jit_solution(10792632579092109949)
XLA Ops:
  10.2 2.8 collective-permute-start.1
  14.2 5.4 collective-permute-done.1
  21.4 2.6 fusion.107
  24.0 3.4 collective-permute-done.2
  30.0 4.3 collective-permute-done.3
  34.3 2.3 collective-permute-start.4
  37.7 9.2 collective-permute-done.4
  47.3 2.9 fusion.7
  50.2 2.9 select_bitcast_fusion.7
  53.8 125.0 %all-reduce.6.cloned.1.call-done = f32[1,32,1024]{2,1,0:T(8,128)} async-done(((f32[1,32,1024]{2,1,0:T(8,128)}), f32[1,32,1024]{2,1,0:T(8,128)}) %all-reduce.6.cloned.1.call-update) | async-done | bytes 131088 | tf_op jit(solution)/shard_map/psum | solution.py:37
  178.9 2.9 fusion.52
  181.8 1.9 fusion.51
  183.7 1.9 convolution_subtract_fusion.3
  185.6 1.9 convolution_add_fusion.3
  187.6 1.9 collective-permute-done.5
  191.0 12.5 %collective-permute-done.6 = f32[2,1,32,2048]{3,2,1,0:T(8,128)S(1)} collective-permute-done((f32[2,1,32,2048]{3,2,1,0:T(8,128)S(1)}, f32[2,1,32,2048]{3,2,1,0:T(8,128)S(1)}, u32[]{:S(2)}, u32[]{:S(2)}) %collective-permute-start.6) | collective-permute-done | bytes 524320 | tf_op jit(solution)/shard_map/ppermute | solution.py:11
  204.9 11.6 %collective-permute-done.7 = f32[2,1,32,2048]{3,2,1,0:T(8,128)S(1)} collective-permute-done((f32[2,1,32,2048]{3,2,1,0:T(8,128)S(1)}, f32[2,1,32,2048]{3,2,1,0:T(8,128)S(1)}, u32[]{:S(2)}, u32[]{:S(2)}) %collective-permute-start.7) | collective-permute-done | bytes 524320 | tf_op jit(solution)/shard_map/ppermute | solution.py:11
  218.0 10.8 collective-permute-done.8
  230.3 22.1 %collective-permute-done.9 = f32[2,1,32,2048]{3,2,1,0:T(8,128)S(1)} collective-permute-done((f32[2,1,32,2048]{3,2,1,0:T(8,128)S(1)}, f32[2,1,32,2048]{3,2,1,0:T(8,128)S(1)}, u32[]{:S(2)}, u32[]{:S(2)}) %collective-permute-start.9) | collective-permute-done | bytes 524320 | tf_op jit(solution)/shard_map/ppermute | solution.py:11
  259.4 38.0 %psum.85 = f32[1,32,32]{1,2,0:T(8,128)S(1)} all-reduce(f32[1,32,32]{1,2,0:T(8,128)S(1)} %convolution_bitcast_fusion.10), channel_id=1, replica_groups=mesh['gx'=8,'gy'=4] {'gx','gy'}, use_global_device_ids=true, to_apply=%region_1.2 | all-reduce | flops 1024 | bytes 8192 | tf_op jit(solution)/shard_map/psum | solution.py:118
  297.4 2.9 custom-call.21
  301.7 2.4 custom-call.22
  310.2 125.8 %all-reduce.8.cloned.1.call-done = f32[1,32,1024]{2,1,0:T(8,128)} async-done(((f32[1,32,1024]{2,1,0:T(8,128)}), f32[1,32,1024]{2,1,0:T(8,128)}) %all-reduce.8.cloned.1.call-update) | async-done | bytes 131088 | tf_op jit(solution)/shard_map/psum | solution.py:37
  436.1 2.9 fusion.54
  439.0 1.9 fusion.53
  440.9 1.9 convolution_subtract_fusion.2
  442.8 1.9 convolution_add_fusion.2
  444.8 1.9 collective-permute-done.10
  448.2 12.5 %collective-permute-done.11 = f32[2,1,32,2048]{3,2,1,0:T(8,128)S(1)} collective-permute-done((f32[2,1,32,2048]{3,2,1,0:T(8,128)S(1)}, f32[2,1,32,2048]{3,2,1,0:T(8,128)S(1)}, u32[]{:S(2)}, u32[]{:S(2)}) %collective-permute-start.11) | collective-permute-done | bytes 524320 | tf_op jit(solution)/shard_map/ppermute | solution.py:11
  462.1 11.6 %collective-permute-done.12 = f32[2,1,32,2048]{3,2,1,0:T(8,128)S(1)} collective-permute-done((f32[2,1,32,2048]{3,2,1,0:T(8,128)S(1)}, f32[2,1,32,2048]{3,2,1,0:T(8,128)S(1)}, u32[]{:S(2)}, u32[]{:S(2)}) %collective-permute-start.12) | collective-permute-done | bytes 524320 | tf_op jit(solution)/shard_map/ppermute | solution.py:11
  475.3 10.8 collective-permute-done.13
  487.5 22.1 %collective-permute-done.14 = f32[2,1,32,2048]{3,2,1,0:T(8,128)S(1)} collective-permute-done((f32[2,1,32,2048]{3,2,1,0:T(8,128)S(1)}, f32[2,1,32,2048]{3,2,1,0:T(8,128)S(1)}, u32[]{:S(2)}, u32[]{:S(2)}) %collective-permute-start.14) | collective-permute-done | bytes 524320 | tf_op jit(solution)/shard_map/ppermute | solution.py:11
  516.6 38.1 %psum.87 = f32[1,32,32]{1,2,0:T(8,128)S(1)} all-reduce(f32[1,32,32]{1,2,0:T(8,128)S(1)} %convolution_bitcast_fusion.9), channel_id=1, replica_groups=mesh['gx'=8,'gy'=4] {'gx','gy'}, use_global_device_ids=true, to_apply=%region_5.8 | all-reduce | flops 1024 | bytes 8192 | tf_op jit(solution)/shard_map/psum | solution.py:118
  554.7 2.9 custom-call.23
  559.0 2.4 custom-call.24
  567.5 125.8 %all-reduce.10.cloned.1.call-done = f32[1,32,1024]{2,1,0:T(8,128)} async-done(((f32[1,32,1024]{2,1,0:T(8,128)}), f32[1,32,1024]{2,1,0:T(8,128)}) %all-reduce.10.cloned.1.call-update) | async-done | bytes 131088 | tf_op jit(solution)/shard_map/psum | solution.py:37
  693.3 2.9 fusion.56
  696.2 1.9 fusion.55
  698.1 1.9 convolution_subtract_fusion.1
  700.0 1.9 convolution_add_fusion.1
  702.0 1.9 collective-permute-done.15
  705.4 12.5 %collective-permute-done.16 = f32[2,1,32,2048]{3,2,1,0:T(8,128)S(1)} collective-permute-done((f32[2,1,32,2048]{3,2,1,0:T(8,128)S(1)}, f32[2,1,32,2048]{3,2,1,0:T(8,128)S(1)}, u32[]{:S(2)}, u32[]{:S(2)}) %collective-permute-start.16) | collective-permute-done | bytes 524320 | tf_op jit(solution)/shard_map/ppermute | solution.py:11
  719.4 11.6 %collective-permute-done.17 = f32[2,1,32,2048]{3,2,1,0:T(8,128)S(1)} collective-permute-done((f32[2,1,32,2048]{3,2,1,0:T(8,128)S(1)}, f32[2,1,32,2048]{3,2,1,0:T(8,128)S(1)}, u32[]{:S(2)}, u32[]{:S(2)}) %collective-permute-start.17) | collective-permute-done | bytes 524320 | tf_op jit(solution)/shard_map/ppermute | solution.py:11
  732.5 10.8 collective-permute-done.18
  744.7 22.1 %collective-permute-done.19 = f32[2,1,32,2048]{3,2,1,0:T(8,128)S(1)} collective-permute-done((f32[2,1,32,2048]{3,2,1,0:T(8,128)S(1)}, f32[2,1,32,2048]{3,2,1,0:T(8,128)S(1)}, u32[]{:S(2)}, u32[]{:S(2)}) %collective-permute-start.19) | collective-permute-done | bytes 524320 | tf_op jit(solution)/shard_map/ppermute | solution.py:11
  773.8 38.2 %psum.89 = f32[1,32,32]{1,2,0:T(8,128)S(1)} all-reduce(f32[1,32,32]{1,2,0:T(8,128)S(1)} %convolution_bitcast_fusion.8), channel_id=1, replica_groups=mesh['gx'=8,'gy'=4] {'gx','gy'}, use_global_device_ids=true, to_apply=%region_7.10 | all-reduce | flops 1024 | bytes 8192 | tf_op jit(solution)/shard_map/psum | solution.py:118
  812.1 2.9 custom-call.25
  816.4 2.4 custom-call.26
  824.9 125.8 %all-reduce.12.cloned.1.call-done = f32[1,32,1024]{2,1,0:T(8,128)} async-done(((f32[1,32,1024]{2,1,0:T(8,128)}), f32[1,32,1024]{2,1,0:T(8,128)}) %all-reduce.12.cloned.1.call-update) | async-done | bytes 131088 | tf_op jit(solution)/shard_map/psum | solution.py:37
  950.7 2.9 fusion.58
  955.5 1.9 convolution_subtract_fusion
  957.4 1.9 convolution_add_fusion
  959.5 1.9 collective-permute-done.20
  962.8 12.5 %collective-permute-done.21 = f32[2,1,32,2048]{3,2,1,0:T(8,128)S(1)} collective-permute-done((f32[2,1,32,2048]{3,2,1,0:T(8,128)S(1)}, f32[2,1,32,2048]{3,2,1,0:T(8,128)S(1)}, u32[]{:S(2)}, u32[]{:S(2)}) %collective-permute-start.21) | collective-permute-done | bytes 524320 | tf_op jit(solution)/shard_map/ppermute | solution.py:11
  976.8 11.6 %collective-permute-done.22 = f32[2,1,32,2048]{3,2,1,0:T(8,128)S(1)} collective-permute-done((f32[2,1,32,2048]{3,2,1,0:T(8,128)S(1)}, f32[2,1,32,2048]{3,2,1,0:T(8,128)S(1)}, u32[]{:S(2)}, u32[]{:S(2)}) %collective-permute-start.22) | collective-permute-done | bytes 524320 | tf_op jit(solution)/shard_map/ppermute | solution.py:11
  989.9 10.8 collective-permute-done.23
  1002.2 22.0 %collective-permute-done.24 = f32[2,1,32,2048]{3,2,1,0:T(8,128)S(1)} collective-permute-done((f32[2,1,32,2048]{3,2,1,0:T(8,128)S(1)}, f32[2,1,32,2048]{3,2,1,0:T(8,128)S(1)}, u32[]{:S(2)}, u32[]{:S(2)}) %collective-permute-start.24) | collective-permute-done | bytes 524320 | tf_op jit(solution)/shard_map/ppermute | solution.py:11
  1026.1 38.0 %psum.91 = f32[1,32,32]{1,2,0:T(8,128)S(1)} all-reduce(f32[1,32,32]{1,2,0:T(8,128)S(1)} %convolution_bitcast_fusion.7), channel_id=1, replica_groups=mesh['gx'=8,'gy'=4] {'gx','gy'}, use_global_device_ids=true, to_apply=%region_9.12 | all-reduce | flops 1024 | bytes 8192 | tf_op jit(solution)/shard_map/psum | solution.py:118
  1064.2 2.9 custom-call.27
  1068.5 2.4 custom-call.28
  1075.8 12.2 %collective-permute-done.26 = f32[1,32,32,1]{3,1,2,0:T(8,128)S(1)} collective-permute-done((f32[1,32,32,1]{3,1,2,0:T(8,128)S(1)}, f32[1,32,32,1]{3,1,2,0:T(8,128)S(1)}, u32[]{:S(2)}, u32[]{:S(2)}) %collective-permute-start.26) | collective-permute-done | bytes 4128 | tf_op jit(solution)/shard_map/ppermute | solution.py:17
  1091.3 40.9 %all-reduce = (f32[1,1,32,32]{2,3,1,0:T(8,128)S(1)}, f32[1,1,32,32]{2,3,1,0:T(8,128)S(1)}, f32[1,1,32,32]{3,2,1,0:T(8,128)S(1)}, f32[1,1,32,32]{3,2,1,0:T(8,128)S(1)}) all-reduce(f32[1,1,32,32]{2,3,1,0:T(8,128)S(1)} %convolution_bitcast_fusion.5, ...), channel_id=1, replica_groups=mesh['gx'=8,'gy'=4] {'gx','gy'}, use_global_device_ids=true, to_apply=%region_10.13 | all-reduce | flops 4096 | bytes 32768 | tf_op jit(solution)/shard_map/psum | solution.py:124
  1132.4 5.9 custom-call.13
  1138.5 4.9 custom-call.14
  (175 shorter events, 93.0 us)
Async XLA Ops:
  7.2 171.7 %all-reduce.6.cloned.1.call-start = ((), (), s32[]{:S(2)}) async-start(), calls=%async_computation | async-start | bytes 262144 | tf_op jit(solution)/shard_map/psum | solution.py:37
  8.4 1.7 collective-permute-start
  10.2 9.5 collective-permute-start.1
  19.6 7.8 collective-permute-start.2
  24.0 13.7 %copy-start = (bf16[1,1,32,64,512]{4,3,2,1,0:T(8,128)(2,1)}, bf16[1,1,32,64,512]{4,3,2,1,0:T(8,128)(2,1)S(1)}, u32[]{:S(2)}) copy-start(bf16[1,1,32,64,512]{4,3,2,1,0:T(8,128)(2,1)S(1)} %get-tuple-element.15) | copy-start | bytes 6291460
  27.4 6.9 collective-permute-start.3
  34.3 12.6 %collective-permute-start.4 = (f32[1,1,32,2048]{3,2,1,0:T(8,128)S(1)}, f32[1,1,32,2048]{3,2,1,0:T(8,128)S(1)}, u32[]{:S(2)}, u32[]{:S(2)}) collective-permute-start(f32[1,1,32,2048]{3,2,1,0:T(8,128)S(1)} %collective-permute-done.3), channel_id=1, source_target_pairs={{0,2},{1,3},{2,0},{3,1},{4,6},{5,7},{6,4},{7,5},{8,10},{9,11},{10,... | collective-permute-start | bytes 786440 | tf_op jit(solution)/shard_map/ppermute | solution.py:11
  53.8 382.3 %all-reduce.8.cloned.1.call-start = ((), (), s32[]{:S(2)}) async-start(), calls=%async_computation.1 | async-start | bytes 262144 | tf_op jit(solution)/shard_map/psum | solution.py:37
  178.9 2.9 copy-start.1
  178.9 2.9 copy-start.8
  187.5 2.0 collective-permute-start.5
  189.5 14.0 %collective-permute-start.6 = (f32[2,1,32,2048]{3,2,1,0:T(8,128)S(1)}, f32[2,1,32,2048]{3,2,1,0:T(8,128)S(1)}, u32[]{:S(2)}, u32[]{:S(2)}) collective-permute-start(f32[2,1,32,2048]{3,2,1,0:T(8,128)S(1)} %collective-permute-done.5), channel_id=1, source_target_pairs={{0,8},{4,12},{8,0},{12,4},{16,24},{20,28},{24,16},{28,20},{1,9},{5... | collective-permute-start | bytes 1572872 | tf_op jit(solution)/shard_map/ppermute | solution.py:11
  203.5 13.1 %collective-permute-start.7 = (f32[2,1,32,2048]{3,2,1,0:T(8,128)S(1)}, f32[2,1,32,2048]{3,2,1,0:T(8,128)S(1)}, u32[]{:S(2)}, u32[]{:S(2)}) collective-permute-start(f32[2,1,32,2048]{3,2,1,0:T(8,128)S(1)} %collective-permute-done.6), channel_id=1, source_target_pairs={{0,16},{4,20},{8,24},{12,28},{16,0},{20,4},{24,8},{28,12},{1,17},{... | collective-permute-start | bytes 1572872 | tf_op jit(solution)/shard_map/ppermute | solution.py:11
  216.6 12.3 %collective-permute-start.8 = (f32[2,1,32,2048]{3,2,1,0:T(8,128)S(1)}, f32[2,1,32,2048]{3,2,1,0:T(8,128)S(1)}, u32[]{:S(2)}, u32[]{:S(2)}) collective-permute-start(f32[2,1,32,2048]{3,2,1,0:T(8,128)S(1)} %collective-permute-done.7), channel_id=1, source_target_pairs={{0,1},{1,0},{2,3},{3,2},{4,5},{5,4},{6,7},{7,6},{8,9},{9,8},{10,11... | collective-permute-start | bytes 1572872 | tf_op jit(solution)/shard_map/ppermute | solution.py:11
  228.8 23.5 %collective-permute-start.9 = (f32[2,1,32,2048]{3,2,1,0:T(8,128)S(1)}, f32[2,1,32,2048]{3,2,1,0:T(8,128)S(1)}, u32[]{:S(2)}, u32[]{:S(2)}) collective-permute-start(f32[2,1,32,2048]{3,2,1,0:T(8,128)S(1)} %collective-permute-done.8), channel_id=1, source_target_pairs={{0,2},{1,3},{2,0},{3,1},{4,6},{5,7},{6,4},{7,5},{8,10},{9,11},{10,... | collective-permute-start | bytes 1572872 | tf_op jit(solution)/shard_map/ppermute | solution.py:11
  304.4 1.8 copy-start.2
  310.2 383.1 %all-reduce.10.cloned.1.call-start = ((), (), s32[]{:S(2)}) async-start(), calls=%async_computation.2 | async-start | bytes 262144 | tf_op jit(solution)/shard_map/psum | solution.py:37
  436.1 2.9 copy-start.3
  436.1 2.9 copy-start.9
  444.7 2.0 collective-permute-start.10
  446.7 14.0 %collective-permute-start.11 = (f32[2,1,32,2048]{3,2,1,0:T(8,128)S(1)}, f32[2,1,32,2048]{3,2,1,0:T(8,128)S(1)}, u32[]{:S(2)}, u32[]{:S(2)}) collective-permute-start(f32[2,1,32,2048]{3,2,1,0:T(8,128)S(1)} %collective-permute-done.10), channel_id=1, source_target_pairs={{0,8},{4,12},{8,0},{12,4},{16,24},{20,28},{24,16},{28,20},{1,9},{5... | collective-permute-start | bytes 1572872 | tf_op jit(solution)/shard_map/ppermute | solution.py:11
  460.7 13.1 %collective-permute-start.12 = (f32[2,1,32,2048]{3,2,1,0:T(8,128)S(1)}, f32[2,1,32,2048]{3,2,1,0:T(8,128)S(1)}, u32[]{:S(2)}, u32[]{:S(2)}) collective-permute-start(f32[2,1,32,2048]{3,2,1,0:T(8,128)S(1)} %collective-permute-done.11), channel_id=1, source_target_pairs={{0,16},{4,20},{8,24},{12,28},{16,0},{20,4},{24,8},{28,12},{1,17},{... | collective-permute-start | bytes 1572872 | tf_op jit(solution)/shard_map/ppermute | solution.py:11
  473.8 12.3 %collective-permute-start.13 = (f32[2,1,32,2048]{3,2,1,0:T(8,128)S(1)}, f32[2,1,32,2048]{3,2,1,0:T(8,128)S(1)}, u32[]{:S(2)}, u32[]{:S(2)}) collective-permute-start(f32[2,1,32,2048]{3,2,1,0:T(8,128)S(1)} %collective-permute-done.12), channel_id=1, source_target_pairs={{0,1},{1,0},{2,3},{3,2},{4,5},{5,4},{6,7},{7,6},{8,9},{9,8},{10,11... | collective-permute-start | bytes 1572872 | tf_op jit(solution)/shard_map/ppermute | solution.py:11
  486.0 23.5 %collective-permute-start.14 = (f32[2,1,32,2048]{3,2,1,0:T(8,128)S(1)}, f32[2,1,32,2048]{3,2,1,0:T(8,128)S(1)}, u32[]{:S(2)}, u32[]{:S(2)}) collective-permute-start(f32[2,1,32,2048]{3,2,1,0:T(8,128)S(1)} %collective-permute-done.13), channel_id=1, source_target_pairs={{0,2},{1,3},{2,0},{3,1},{4,6},{5,7},{6,4},{7,5},{8,10},{9,11},{10,... | collective-permute-start | bytes 1572872 | tf_op jit(solution)/shard_map/ppermute | solution.py:11
  561.6 1.8 copy-start.4
  567.5 383.3 %all-reduce.12.cloned.1.call-start = ((), (), s32[]{:S(2)}) async-start(), calls=%async_computation.3 | async-start | bytes 262144 | tf_op jit(solution)/shard_map/psum | solution.py:37
  693.3 2.9 copy-start.5
  693.3 2.9 copy-start.10
  702.0 2.0 collective-permute-start.15
  703.9 14.0 %collective-permute-start.16 = (f32[2,1,32,2048]{3,2,1,0:T(8,128)S(1)}, f32[2,1,32,2048]{3,2,1,0:T(8,128)S(1)}, u32[]{:S(2)}, u32[]{:S(2)}) collective-permute-start(f32[2,1,32,2048]{3,2,1,0:T(8,128)S(1)} %collective-permute-done.15), channel_id=1, source_target_pairs={{0,8},{4,12},{8,0},{12,4},{16,24},{20,28},{24,16},{28,20},{1,9},{5... | collective-permute-start | bytes 1572872 | tf_op jit(solution)/shard_map/ppermute | solution.py:11
  717.9 13.1 %collective-permute-start.17 = (f32[2,1,32,2048]{3,2,1,0:T(8,128)S(1)}, f32[2,1,32,2048]{3,2,1,0:T(8,128)S(1)}, u32[]{:S(2)}, u32[]{:S(2)}) collective-permute-start(f32[2,1,32,2048]{3,2,1,0:T(8,128)S(1)} %collective-permute-done.16), channel_id=1, source_target_pairs={{0,16},{4,20},{8,24},{12,28},{16,0},{20,4},{24,8},{28,12},{1,17},{... | collective-permute-start | bytes 1572872 | tf_op jit(solution)/shard_map/ppermute | solution.py:11
  731.0 12.3 %collective-permute-start.18 = (f32[2,1,32,2048]{3,2,1,0:T(8,128)S(1)}, f32[2,1,32,2048]{3,2,1,0:T(8,128)S(1)}, u32[]{:S(2)}, u32[]{:S(2)}) collective-permute-start(f32[2,1,32,2048]{3,2,1,0:T(8,128)S(1)} %collective-permute-done.17), channel_id=1, source_target_pairs={{0,1},{1,0},{2,3},{3,2},{4,5},{5,4},{6,7},{7,6},{8,9},{9,8},{10,11... | collective-permute-start | bytes 1572872 | tf_op jit(solution)/shard_map/ppermute | solution.py:11
  743.3 23.5 %collective-permute-start.19 = (f32[2,1,32,2048]{3,2,1,0:T(8,128)S(1)}, f32[2,1,32,2048]{3,2,1,0:T(8,128)S(1)}, u32[]{:S(2)}, u32[]{:S(2)}) collective-permute-start(f32[2,1,32,2048]{3,2,1,0:T(8,128)S(1)} %collective-permute-done.18), channel_id=1, source_target_pairs={{0,2},{1,3},{2,0},{3,1},{4,6},{5,7},{6,4},{7,5},{8,10},{9,11},{10,... | collective-permute-start | bytes 1572872 | tf_op jit(solution)/shard_map/ppermute | solution.py:11
  819.1 1.8 copy-start.6
  950.7 2.9 copy-start.7
  950.7 2.9 copy-start.11
  959.4 2.0 collective-permute-start.20
  961.4 14.0 %collective-permute-start.21 = (f32[2,1,32,2048]{3,2,1,0:T(8,128)S(1)}, f32[2,1,32,2048]{3,2,1,0:T(8,128)S(1)}, u32[]{:S(2)}, u32[]{:S(2)}) collective-permute-start(f32[2,1,32,2048]{3,2,1,0:T(8,128)S(1)} %collective-permute-done.20), channel_id=1, source_target_pairs={{0,8},{4,12},{8,0},{12,4},{16,24},{20,28},{24,16},{28,20},{1,9},{5... | collective-permute-start | bytes 1572872 | tf_op jit(solution)/shard_map/ppermute | solution.py:11
  975.3 13.1 %collective-permute-start.22 = (f32[2,1,32,2048]{3,2,1,0:T(8,128)S(1)}, f32[2,1,32,2048]{3,2,1,0:T(8,128)S(1)}, u32[]{:S(2)}, u32[]{:S(2)}) collective-permute-start(f32[2,1,32,2048]{3,2,1,0:T(8,128)S(1)} %collective-permute-done.21), channel_id=1, source_target_pairs={{0,16},{4,20},{8,24},{12,28},{16,0},{20,4},{24,8},{28,12},{1,17},{... | collective-permute-start | bytes 1572872 | tf_op jit(solution)/shard_map/ppermute | solution.py:11
  988.4 12.3 %collective-permute-start.23 = (f32[2,1,32,2048]{3,2,1,0:T(8,128)S(1)}, f32[2,1,32,2048]{3,2,1,0:T(8,128)S(1)}, u32[]{:S(2)}, u32[]{:S(2)}) collective-permute-start(f32[2,1,32,2048]{3,2,1,0:T(8,128)S(1)} %collective-permute-done.22), channel_id=1, source_target_pairs={{0,1},{1,0},{2,3},{3,2},{4,5},{5,4},{6,7},{7,6},{8,9},{9,8},{10,11... | collective-permute-start | bytes 1572872 | tf_op jit(solution)/shard_map/ppermute | solution.py:11
  1000.7 23.5 %collective-permute-start.24 = (f32[2,1,32,2048]{3,2,1,0:T(8,128)S(1)}, f32[2,1,32,2048]{3,2,1,0:T(8,128)S(1)}, u32[]{:S(2)}, u32[]{:S(2)}) collective-permute-start(f32[2,1,32,2048]{3,2,1,0:T(8,128)S(1)} %collective-permute-done.23), channel_id=1, source_target_pairs={{0,2},{1,3},{2,0},{3,1},{4,6},{5,7},{6,4},{7,5},{8,10},{9,11},{10,... | collective-permute-start | bytes 1572872 | tf_op jit(solution)/shard_map/ppermute | solution.py:11
  1072.0 15.9 %collective-permute-start.26 = (f32[1,32,32,1]{3,1,2,0:T(8,128)S(1)}, f32[1,32,32,1]{3,1,2,0:T(8,128)S(1)}, u32[]{:S(2)}, u32[]{:S(2)}) collective-permute-start(f32[1,32,32,1]{3,1,2,0:T(8,128)S(1)} %bitcast.338), channel_id=1, source_target_pairs={{1,0},{2,1},{3,2},{5,4},{6,5},{7,6},{9,8},{10,9},{11,10},{13,12},{... | collective-permute-start | bytes 12296 | tf_op jit(solution)/shard_map/ppermute | solution.py:17
  1074.5 15.5 %collective-permute-start.25 = (f32[1,32,1,64]{3,1,2,0:T(8,128)S(1)}, f32[1,32,1,64]{3,1,2,0:T(8,128)S(1)}, u32[]{:S(2)}, u32[]{:S(2)}) collective-permute-start(f32[1,32,1,64]{3,1,2,0:T(8,128)S(1)} %slice.232), channel_id=1, source_target_pairs={{4,0},{8,4},{12,8},{16,12},{20,16},{24,20},{28,24},{5,1},{9,5},{13... | collective-permute-start | bytes 24584 | tf_op jit(solution)/shard_map/ppermute | solution.py:17
Sparse Core Ops, SparseCore 0:
  53.9 124.9 all-reduce.5
  310.3 125.6 all-reduce.7
  567.6 125.6 all-reduce.9
  825.0 125.6 all-reduce.11
where the time goes:
time: 1160 us; the launch traced here: 1150 us
  waiting for transfers between devices  774 us (67%)
  blocking collectives  193 us (17%)
  matrix products  65.3 us (6%)
  other arithmetic  40.8 us (4%)
  starting transfers between devices  35.6 us (3%)
  local copies, waits for them, and re-layouts  28.2 us (2%)
  between operations  14.8 us (1%)
    psum x4, waiting for transfers between devices, project(): return lax.psum(local_side, ('gx', 'gy'))  502 us
    ppermute x25, waiting for transfers between devices, swapped(): lax.ppermute(x, axis, [(i, i ^ 1 << apart) for i in range(lax.axis_size(a...  259 us
    psum x4, blocking collectives, body(): gram = lax.psum(gram_of(grown), ('gx', 'gy'))  152 us
    psum x1, blocking collectives, body(): lax.psum((local_terms[0], local_terms[1], local_terms[2], local_terms[3])...  40.9 us
    ppermute x25, starting transfers between devices, swapped(): lax.ppermute(x, axis, [(i, i ^ 1 << apart) for i in range(lax.axis_size(a...  32.9 us
  transfers between devices with their start and end apart: 31, of which 30 were waited for; matrix products, arithmetic and copies ran while one was open for 1% of the time, Pallas kernels for 0%

commit v1 on v0

--- a/solution.py
+++ b/solution.py
@@ -34,7 +34,7 @@
 
 
 def project(local_side):
-    return lax.psum(local_side, ("gx", "gy"))
+    return lax.psum(lax.psum(local_side, "gy"), "gx")
 
 
 def gram_of(grown):

time: 1160 us -> 1030 us (0.89)
  waiting for transfers between devices: 774 us -> 638 us
    psum x4 -> x8, waiting for transfers between devices: 502 us -> 366 us  [project(): return lax.psum(lax.psum(local_side, 'gy'), 'gx')]
  transfers between devices with their start and end apart: 31 -> 35, of which waited for: 30 -> 34; matrix products, arithmetic and copies ran while one was open for 1% -> 1% of each run, Pallas kernels for 0% -> 0%
where the time goes in v1:
time: 1030 us; the launch traced here: 1020 us
  waiting for transfers between devices  638 us (62%)
  blocking collectives  197 us (19%)
  matrix products  65.3 us (6%)
  other arithmetic  40.8 us (4%)
  starting transfers between devices  34.5 us (3%)
  local copies, waits for them, and re-layouts  28.2 us (3%)
  between operations  15.2 us (1%)
    psum x8, waiting for transfers between devices, project(): return lax.psum(lax.psum(local_side, 'gy'), 'gx')  366 us
    ppermute x25, waiting for transfers between devices, swapped(): lax.ppermute(x, axis, [(i, i ^ 1 << apart) for i in range(lax.axis_size(a...  260 us
    psum x4, blocking collectives, body(): gram = lax.psum(gram_of(grown), ('gx', 'gy'))  156 us
    psum x1, blocking collectives, body(): lax.psum((local_terms[0], local_terms[1], local_terms[2], local_terms[3])...  41 us
    ppermute x25, starting transfers between devices, swapped(): lax.ppermute(x, axis, [(i, i ^ 1 << apart) for i in range(lax.axis_size(a...  31.7 us
  transfers between devices with their start and end apart: 35, of which 34 were waited for; matrix products, arithmetic and copies ran while one was open for 1% of the time, Pallas kernels for 0%

profile of v1, /device:TPU:0, one launch (start us, length us, event | category | flops | bytes accessed | tf_op | source)
XLA Modules:
  0.0 1018.3 jit_solution(3443632294313039356)
XLA Ops:
  10.2 2.8 collective-permute-start.1
  14.2 5.4 collective-permute-done.1
  21.4 2.6 fusion.107
  24.0 3.4 collective-permute-done.2
  30.0 4.3 collective-permute-done.3
  34.3 2.3 collective-permute-start.4
  37.7 9.2 collective-permute-done.4
  47.3 2.9 fusion.7
  50.2 2.9 select_bitcast_fusion.7
  53.8 35.3 %all-reduce.10.cloned.1.call-done = f32[1,32,1024]{2,1,0:T(8,128)} async-done(((f32[1,32,1024]{2,1,0:T(8,128)}), f32[1,32,1024]{2,1,0:T(8,128)}) %all-reduce.10.cloned.1.call-update) | async-done | bytes 131088 | tf_op jit(solution)/shard_map/psum | solution.py:37
  89.2 56.1 %all-reduce.12.cloned.1.call-done = f32[1,32,1024]{2,1,0:T(8,128)} async-done(((f32[1,32,1024]{2,1,0:T(8,128)}), f32[1,32,1024]{2,1,0:T(8,128)}) %all-reduce.12.cloned.1.call-update) | async-done | bytes 131088 | tf_op jit(solution)/shard_map/psum | solution.py:37
  145.3 2.9 fusion.52
  150.1 1.9 convolution_subtract_fusion.3
  152.0 1.9 convolution_add_fusion.3
  156.8 13.1 %collective-permute-done.6 = f32[2,1,32,2048]{3,2,1,0:T(8,128)S(1)} collective-permute-done((f32[2,1,32,2048]{3,2,1,0:T(8,128)S(1)}, f32[2,1,32,2048]{3,2,1,0:T(8,128)S(1)}, u32[]{:S(2)}, u32[]{:S(2)}) %collective-permute-start.6) | collective-permute-done | bytes 524320 | tf_op jit(solution)/shard_map/ppermute | solution.py:11
  170.8 12.3 %collective-permute-done.7 = f32[2,1,32,2048]{3,2,1,0:T(8,128)S(1)} collective-permute-done((f32[2,1,32,2048]{3,2,1,0:T(8,128)S(1)}, f32[2,1,32,2048]{3,2,1,0:T(8,128)S(1)}, u32[]{:S(2)}, u32[]{:S(2)}) %collective-permute-start.7) | collective-permute-done | bytes 524320 | tf_op jit(solution)/shard_map/ppermute | solution.py:11
  184.5 10.8 %collective-permute-done.8 = f32[2,1,32,2048]{3,2,1,0:T(8,128)S(1)} collective-permute-done((f32[2,1,32,2048]{3,2,1,0:T(8,128)S(1)}, f32[2,1,32,2048]{3,2,1,0:T(8,128)S(1)}, u32[]{:S(2)}, u32[]{:S(2)}) %collective-permute-start.8) | collective-permute-done | bytes 524320 | tf_op jit(solution)/shard_map/ppermute | solution.py:11
  195.3 2.4 collective-permute-start.9
  197.7 21.1 %collective-permute-done.9 = f32[2,1,32,2048]{3,2,1,0:T(8,128)S(1)} collective-permute-done((f32[2,1,32,2048]{3,2,1,0:T(8,128)S(1)}, f32[2,1,32,2048]{3,2,1,0:T(8,128)S(1)}, u32[]{:S(2)}, u32[]{:S(2)}) %collective-permute-start.9) | collective-permute-done | bytes 524320 | tf_op jit(solution)/shard_map/ppermute | solution.py:11
  225.8 38.9 %psum.114 = f32[1,32,32]{1,2,0:T(8,128)S(1)} all-reduce(f32[1,32,32]{1,2,0:T(8,128)S(1)} %convolution_bitcast_fusion.10), channel_id=1, replica_groups=mesh['gx'=8,'gy'=4] {'gx','gy'}, use_global_device_ids=true, to_apply=%region_2.3 | all-reduce | flops 1024 | bytes 8192 | tf_op jit(solution)/shard_map/psum | solution.py:118
  264.7 2.9 custom-call.21
  269.0 2.4 custom-call.22
  277.6 35.5 %all-reduce.14.cloned.1.call-done = f32[1,32,1024]{2,1,0:T(8,128)} async-done(((f32[1,32,1024]{2,1,0:T(8,128)}), f32[1,32,1024]{2,1,0:T(8,128)}) %all-reduce.14.cloned.1.call-update) | async-done | bytes 131088 | tf_op jit(solution)/shard_map/psum | solution.py:37
  313.1 56.0 %all-reduce.16.cloned.1.call-done = f32[1,32,1024]{2,1,0:T(8,128)} async-done(((f32[1,32,1024]{2,1,0:T(8,128)}), f32[1,32,1024]{2,1,0:T(8,128)}) %all-reduce.16.cloned.1.call-update) | async-done | bytes 131088 | tf_op jit(solution)/shard_map/psum | solution.py:37
  369.1 2.9 fusion.54
  373.9 1.9 convolution_subtract_fusion.2
  375.8 1.9 convolution_add_fusion.2
  380.6 13.1 %collective-permute-done.11 = f32[2,1,32,2048]{3,2,1,0:T(8,128)S(1)} collective-permute-done((f32[2,1,32,2048]{3,2,1,0:T(8,128)S(1)}, f32[2,1,32,2048]{3,2,1,0:T(8,128)S(1)}, u32[]{:S(2)}, u32[]{:S(2)}) %collective-permute-start.11) | collective-permute-done | bytes 524320 | tf_op jit(solution)/shard_map/ppermute | solution.py:11
  394.6 12.3 %collective-permute-done.12 = f32[2,1,32,2048]{3,2,1,0:T(8,128)S(1)} collective-permute-done((f32[2,1,32,2048]{3,2,1,0:T(8,128)S(1)}, f32[2,1,32,2048]{3,2,1,0:T(8,128)S(1)}, u32[]{:S(2)}, u32[]{:S(2)}) %collective-permute-start.12) | collective-permute-done | bytes 524320 | tf_op jit(solution)/shard_map/ppermute | solution.py:11
  408.3 10.8 %collective-permute-done.13 = f32[2,1,32,2048]{3,2,1,0:T(8,128)S(1)} collective-permute-done((f32[2,1,32,2048]{3,2,1,0:T(8,128)S(1)}, f32[2,1,32,2048]{3,2,1,0:T(8,128)S(1)}, u32[]{:S(2)}, u32[]{:S(2)}) %collective-permute-start.13) | collective-permute-done | bytes 524320 | tf_op jit(solution)/shard_map/ppermute | solution.py:11
  419.1 2.4 collective-permute-start.14
  421.5 21.1 %collective-permute-done.14 = f32[2,1,32,2048]{3,2,1,0:T(8,128)S(1)} collective-permute-done((f32[2,1,32,2048]{3,2,1,0:T(8,128)S(1)}, f32[2,1,32,2048]{3,2,1,0:T(8,128)S(1)}, u32[]{:S(2)}, u32[]{:S(2)}) %collective-permute-start.14) | collective-permute-done | bytes 524320 | tf_op jit(solution)/shard_map/ppermute | solution.py:11
  449.6 38.9 %psum.117 = f32[1,32,32]{1,2,0:T(8,128)S(1)} all-reduce(f32[1,32,32]{1,2,0:T(8,128)S(1)} %convolution_bitcast_fusion.9), channel_id=1, replica_groups=mesh['gx'=8,'gy'=4] {'gx','gy'}, use_global_device_ids=true, to_apply=%region_7.10 | all-reduce | flops 1024 | bytes 8192 | tf_op jit(solution)/shard_map/psum | solution.py:118
  488.6 2.9 custom-call.23
  492.8 2.4 custom-call.24
  501.4 35.5 %all-reduce.18.cloned.1.call-done = f32[1,32,1024]{2,1,0:T(8,128)} async-done(((f32[1,32,1024]{2,1,0:T(8,128)}), f32[1,32,1024]{2,1,0:T(8,128)}) %all-reduce.18.cloned.1.call-update) | async-done | bytes 131088 | tf_op jit(solution)/shard_map/psum | solution.py:37
  536.9 56.0 %all-reduce.20.cloned.1.call-done = f32[1,32,1024]{2,1,0:T(8,128)} async-done(((f32[1,32,1024]{2,1,0:T(8,128)}), f32[1,32,1024]{2,1,0:T(8,128)}) %all-reduce.20.cloned.1.call-update) | async-done | bytes 131088 | tf_op jit(solution)/shard_map/psum | solution.py:37
  592.9 2.9 fusion.56
  597.7 1.9 convolution_subtract_fusion.1
  604.4 13.1 %collective-permute-done.16 = f32[2,1,32,2048]{3,2,1,0:T(8,128)S(1)} collective-permute-done((f32[2,1,32,2048]{3,2,1,0:T(8,128)S(1)}, f32[2,1,32,2048]{3,2,1,0:T(8,128)S(1)}, u32[]{:S(2)}, u32[]{:S(2)}) %collective-permute-start.16) | collective-permute-done | bytes 524320 | tf_op jit(solution)/shard_map/ppermute | solution.py:11
  618.4 12.3 %collective-permute-done.17 = f32[2,1,32,2048]{3,2,1,0:T(8,128)S(1)} collective-permute-done((f32[2,1,32,2048]{3,2,1,0:T(8,128)S(1)}, f32[2,1,32,2048]{3,2,1,0:T(8,128)S(1)}, u32[]{:S(2)}, u32[]{:S(2)}) %collective-permute-start.17) | collective-permute-done | bytes 524320 | tf_op jit(solution)/shard_map/ppermute | solution.py:11
  632.1 10.8 %collective-permute-done.18 = f32[2,1,32,2048]{3,2,1,0:T(8,128)S(1)} collective-permute-done((f32[2,1,32,2048]{3,2,1,0:T(8,128)S(1)}, f32[2,1,32,2048]{3,2,1,0:T(8,128)S(1)}, u32[]{:S(2)}, u32[]{:S(2)}) %collective-permute-start.18) | collective-permute-done | bytes 524320 | tf_op jit(solution)/shard_map/ppermute | solution.py:11
  642.9 2.4 collective-permute-start.19
  645.3 21.1 %collective-permute-done.19 = f32[2,1,32,2048]{3,2,1,0:T(8,128)S(1)} collective-permute-done((f32[2,1,32,2048]{3,2,1,0:T(8,128)S(1)}, f32[2,1,32,2048]{3,2,1,0:T(8,128)S(1)}, u32[]{:S(2)}, u32[]{:S(2)}) %collective-permute-start.19) | collective-permute-done | bytes 524320 | tf_op jit(solution)/shard_map/ppermute | solution.py:11
  673.4 39.1 %psum.120 = f32[1,32,32]{1,2,0:T(8,128)S(1)} all-reduce(f32[1,32,32]{1,2,0:T(8,128)S(1)} %convolution_bitcast_fusion.8), channel_id=1, replica_groups=mesh['gx'=8,'gy'=4] {'gx','gy'}, use_global_device_ids=true, to_apply=%region_10.13 | all-reduce | flops 1024 | bytes 8192 | tf_op jit(solution)/shard_map/psum | solution.py:118
  712.6 2.9 custom-call.25
  716.9 2.4 custom-call.26
  725.4 35.5 %all-reduce.22.cloned.1.call-done = f32[1,32,1024]{2,1,0:T(8,128)} async-done(((f32[1,32,1024]{2,1,0:T(8,128)}), f32[1,32,1024]{2,1,0:T(8,128)}) %all-reduce.22.cloned.1.call-update) | async-done | bytes 131088 | tf_op jit(solution)/shard_map/psum | solution.py:37
  760.9 56.2 %all-reduce.24.cloned.1.call-done = f32[1,32,1024]{2,1,0:T(8,128)} async-done(((f32[1,32,1024]{2,1,0:T(8,128)}), f32[1,32,1024]{2,1,0:T(8,128)}) %all-reduce.24.cloned.1.call-update) | async-done | bytes 131088 | tf_op jit(solution)/shard_map/psum | solution.py:37
  817.1 2.9 fusion.58
  821.9 1.9 convolution_subtract_fusion
  823.8 1.9 convolution_add_fusion
  828.6 13.1 %collective-permute-done.21 = f32[2,1,32,2048]{3,2,1,0:T(8,128)S(1)} collective-permute-done((f32[2,1,32,2048]{3,2,1,0:T(8,128)S(1)}, f32[2,1,32,2048]{3,2,1,0:T(8,128)S(1)}, u32[]{:S(2)}, u32[]{:S(2)}) %collective-permute-start.21) | collective-permute-done | bytes 524320 | tf_op jit(solution)/shard_map/ppermute | solution.py:11
  842.6 12.3 %collective-permute-done.22 = f32[2,1,32,2048]{3,2,1,0:T(8,128)S(1)} collective-permute-done((f32[2,1,32,2048]{3,2,1,0:T(8,128)S(1)}, f32[2,1,32,2048]{3,2,1,0:T(8,128)S(1)}, u32[]{:S(2)}, u32[]{:S(2)}) %collective-permute-start.22) | collective-permute-done | bytes 524320 | tf_op jit(solution)/shard_map/ppermute | solution.py:11
  856.3 10.8 %collective-permute-done.23 = f32[2,1,32,2048]{3,2,1,0:T(8,128)S(1)} collective-permute-done((f32[2,1,32,2048]{3,2,1,0:T(8,128)S(1)}, f32[2,1,32,2048]{3,2,1,0:T(8,128)S(1)}, u32[]{:S(2)}, u32[]{:S(2)}) %collective-permute-start.23) | collective-permute-done | bytes 524320 | tf_op jit(solution)/shard_map/ppermute | solution.py:11
  867.1 2.4 collective-permute-start.24
  869.5 21.1 %collective-permute-done.24 = f32[2,1,32,2048]{3,2,1,0:T(8,128)S(1)} collective-permute-done((f32[2,1,32,2048]{3,2,1,0:T(8,128)S(1)}, f32[2,1,32,2048]{3,2,1,0:T(8,128)S(1)}, u32[]{:S(2)}, u32[]{:S(2)}) %collective-permute-start.24) | collective-permute-done | bytes 524320 | tf_op jit(solution)/shard_map/ppermute | solution.py:11
  892.5 38.9 %psum.123 = f32[1,32,32]{1,2,0:T(8,128)S(1)} all-reduce(f32[1,32,32]{1,2,0:T(8,128)S(1)} %convolution_bitcast_fusion.7), channel_id=1, replica_groups=mesh['gx'=8,'gy'=4] {'gx','gy'}, use_global_device_ids=true, to_apply=%region_13.16 | all-reduce | flops 1024 | bytes 8192 | tf_op jit(solution)/shard_map/psum | solution.py:118
  931.5 2.9 custom-call.27
  935.7 2.4 custom-call.28
  943.0 11.4 %collective-permute-done.26 = f32[1,32,32,1]{3,1,2,0:T(8,128)S(1)} collective-permute-done((f32[1,32,32,1]{3,1,2,0:T(8,128)S(1)}, f32[1,32,32,1]{3,1,2,0:T(8,128)S(1)}, u32[]{:S(2)}, u32[]{:S(2)}) %collective-permute-start.26) | collective-permute-done | bytes 4128 | tf_op jit(solution)/shard_map/ppermute | solution.py:17
  957.8 41.0 %all-reduce = (f32[1,1,32,32]{2,3,1,0:T(8,128)S(1)}, f32[1,1,32,32]{2,3,1,0:T(8,128)S(1)}, f32[1,1,32,32]{3,2,1,0:T(8,128)S(1)}, f32[1,1,32,32]{3,2,1,0:T(8,128)S(1)}) all-reduce(f32[1,1,32,32]{2,3,1,0:T(8,128)S(1)} %convolution_bitcast_fusion.5, ...), channel_id=1, replica_groups=mesh['gx'=8,'gy'=4] {'gx','gy'}, use_global_device_ids=true, to_apply=%region_14.17 | all-reduce | flops 4096 | bytes 32768 | tf_op jit(solution)/shard_map/psum | solution.py:124
  999.0 5.9 custom-call.13
  1005.1 4.9 custom-call.14
  (187 shorter events, 97.6 us)
Async XLA Ops:
  7.2 81.9 %all-reduce.10.cloned.1.call-start = ((), (), s32[]{:S(2)}) async-start(), calls=%async_computation | async-start | bytes 262144 | tf_op jit(solution)/shard_map/psum | solution.py:37
  8.4 1.7 collective-permute-start
  10.2 9.5 collective-permute-start.1
  19.6 7.8 collective-permute-start.2
  24.0 13.7 %copy-start = (bf16[1,1,32,64,512]{4,3,2,1,0:T(8,128)(2,1)}, bf16[1,1,32,64,512]{4,3,2,1,0:T(8,128)(2,1)S(1)}, u32[]{:S(2)}) copy-start(bf16[1,1,32,64,512]{4,3,2,1,0:T(8,128)(2,1)S(1)} %get-tuple-element.15) | copy-start | bytes 6291460
  27.4 6.9 collective-permute-start.3
  34.3 12.6 %collective-permute-start.4 = (f32[1,1,32,2048]{3,2,1,0:T(8,128)S(1)}, f32[1,1,32,2048]{3,2,1,0:T(8,128)S(1)}, u32[]{:S(2)}, u32[]{:S(2)}) collective-permute-start(f32[1,1,32,2048]{3,2,1,0:T(8,128)S(1)} %collective-permute-done.3), channel_id=1, source_target_pairs={{0,2},{1,3},{2,0},{3,1},{4,6},{5,7},{6,4},{7,5},{8,10},{9,11},{10,... | collective-permute-start | bytes 786440 | tf_op jit(solution)/shard_map/ppermute | solution.py:11
  53.8 91.5 %all-reduce.12.cloned.1.call-start = ((), (), s32[]{:S(2)}) async-start(), calls=%async_computation.1 | async-start | bytes 262144 | tf_op jit(solution)/shard_map/psum | solution.py:37
  89.1 223.9 %all-reduce.14.cloned.1.call-start = ((), (), s32[]{:S(2)}) async-start(), calls=%async_computation.2 | async-start | bytes 262144 | tf_op jit(solution)/shard_map/psum | solution.py:37
  145.3 2.9 copy-start.1
  145.3 2.9 copy-start.8
  154.0 2.0 collective-permute-start.5
  155.9 14.0 %collective-permute-start.6 = (f32[2,1,32,2048]{3,2,1,0:T(8,128)S(1)}, f32[2,1,32,2048]{3,2,1,0:T(8,128)S(1)}, u32[]{:S(2)}, u32[]{:S(2)}) collective-permute-start(f32[2,1,32,2048]{3,2,1,0:T(8,128)S(1)} %collective-permute-done.5), channel_id=1, source_target_pairs={{0,8},{4,12},{8,0},{12,4},{16,24},{20,28},{24,16},{28,20},{1,9},{5... | collective-permute-start | bytes 1572872 | tf_op jit(solution)/shard_map/ppermute | solution.py:11
  169.9 13.1 %collective-permute-start.7 = (f32[2,1,32,2048]{3,2,1,0:T(8,128)S(1)}, f32[2,1,32,2048]{3,2,1,0:T(8,128)S(1)}, u32[]{:S(2)}, u32[]{:S(2)}) collective-permute-start(f32[2,1,32,2048]{3,2,1,0:T(8,128)S(1)} %collective-permute-done.6), channel_id=1, source_target_pairs={{0,16},{4,20},{8,24},{12,28},{16,0},{20,4},{24,8},{28,12},{1,17},{... | collective-permute-start | bytes 1572872 | tf_op jit(solution)/shard_map/ppermute | solution.py:11
  183.0 12.3 %collective-permute-start.8 = (f32[2,1,32,2048]{3,2,1,0:T(8,128)S(1)}, f32[2,1,32,2048]{3,2,1,0:T(8,128)S(1)}, u32[]{:S(2)}, u32[]{:S(2)}) collective-permute-start(f32[2,1,32,2048]{3,2,1,0:T(8,128)S(1)} %collective-permute-done.7), channel_id=1, source_target_pairs={{0,1},{1,0},{2,3},{3,2},{4,5},{5,4},{6,7},{7,6},{8,9},{9,8},{10,11... | collective-permute-start | bytes 1572872 | tf_op jit(solution)/shard_map/ppermute | solution.py:11
  195.3 23.5 %collective-permute-start.9 = (f32[2,1,32,2048]{3,2,1,0:T(8,128)S(1)}, f32[2,1,32,2048]{3,2,1,0:T(8,128)S(1)}, u32[]{:S(2)}, u32[]{:S(2)}) collective-permute-start(f32[2,1,32,2048]{3,2,1,0:T(8,128)S(1)} %collective-permute-done.8), channel_id=1, source_target_pairs={{0,2},{1,3},{2,0},{3,1},{4,6},{5,7},{6,4},{7,5},{8,10},{9,11},{10,... | collective-permute-start | bytes 1572872 | tf_op jit(solution)/shard_map/ppermute | solution.py:11
  271.7 1.8 copy-start.2
  277.5 91.6 %all-reduce.16.cloned.1.call-start = ((), (), s32[]{:S(2)}) async-start(), calls=%async_computation.3 | async-start | bytes 262144 | tf_op jit(solution)/shard_map/psum | solution.py:37
  313.1 223.8 %all-reduce.18.cloned.1.call-start = ((), (), s32[]{:S(2)}) async-start(), calls=%async_computation.4 | async-start | bytes 262144 | tf_op jit(solution)/shard_map/psum | solution.py:37
  369.1 2.9 copy-start.3
  369.1 2.9 copy-start.9
  377.8 2.0 collective-permute-start.10
  379.7 14.0 %collective-permute-start.11 = (f32[2,1,32,2048]{3,2,1,0:T(8,128)S(1)}, f32[2,1,32,2048]{3,2,1,0:T(8,128)S(1)}, u32[]{:S(2)}, u32[]{:S(2)}) collective-permute-start(f32[2,1,32,2048]{3,2,1,0:T(8,128)S(1)} %collective-permute-done.10), channel_id=1, source_target_pairs={{0,8},{4,12},{8,0},{12,4},{16,24},{20,28},{24,16},{28,20},{1,9},{5... | collective-permute-start | bytes 1572872 | tf_op jit(solution)/shard_map/ppermute | solution.py:11
  393.7 13.1 %collective-permute-start.12 = (f32[2,1,32,2048]{3,2,1,0:T(8,128)S(1)}, f32[2,1,32,2048]{3,2,1,0:T(8,128)S(1)}, u32[]{:S(2)}, u32[]{:S(2)}) collective-permute-start(f32[2,1,32,2048]{3,2,1,0:T(8,128)S(1)} %collective-permute-done.11), channel_id=1, source_target_pairs={{0,16},{4,20},{8,24},{12,28},{16,0},{20,4},{24,8},{28,12},{1,17},{... | collective-permute-start | bytes 1572872 | tf_op jit(solution)/shard_map/ppermute | solution.py:11
  406.8 12.3 %collective-permute-start.13 = (f32[2,1,32,2048]{3,2,1,0:T(8,128)S(1)}, f32[2,1,32,2048]{3,2,1,0:T(8,128)S(1)}, u32[]{:S(2)}, u32[]{:S(2)}) collective-permute-start(f32[2,1,32,2048]{3,2,1,0:T(8,128)S(1)} %collective-permute-done.12), channel_id=1, source_target_pairs={{0,1},{1,0},{2,3},{3,2},{4,5},{5,4},{6,7},{7,6},{8,9},{9,8},{10,11... | collective-permute-start | bytes 1572872 | tf_op jit(solution)/shard_map/ppermute | solution.py:11
  419.1 23.5 %collective-permute-start.14 = (f32[2,1,32,2048]{3,2,1,0:T(8,128)S(1)}, f32[2,1,32,2048]{3,2,1,0:T(8,128)S(1)}, u32[]{:S(2)}, u32[]{:S(2)}) collective-permute-start(f32[2,1,32,2048]{3,2,1,0:T(8,128)S(1)} %collective-permute-done.13), channel_id=1, source_target_pairs={{0,2},{1,3},{2,0},{3,1},{4,6},{5,7},{6,4},{7,5},{8,10},{9,11},{10,... | collective-permute-start | bytes 1572872 | tf_op jit(solution)/shard_map/ppermute | solution.py:11
  495.5 1.8 copy-start.4
  501.3 91.6 %all-reduce.20.cloned.1.call-start = ((), (), s32[]{:S(2)}) async-start(), calls=%async_computation.5 | async-start | bytes 262144 | tf_op jit(solution)/shard_map/psum | solution.py:37
  536.9 224.0 %all-reduce.22.cloned.1.call-start = ((), (), s32[]{:S(2)}) async-start(), calls=%async_computation.6 | async-start | bytes 262144 | tf_op jit(solution)/shard_map/psum | solution.py:37
  592.9 2.9 copy-start.5
  592.9 2.9 copy-start.10
  601.6 2.0 collective-permute-start.15
  603.6 14.0 %collective-permute-start.16 = (f32[2,1,32,2048]{3,2,1,0:T(8,128)S(1)}, f32[2,1,32,2048]{3,2,1,0:T(8,128)S(1)}, u32[]{:S(2)}, u32[]{:S(2)}) collective-permute-start(f32[2,1,32,2048]{3,2,1,0:T(8,128)S(1)} %collective-permute-done.15), channel_id=1, source_target_pairs={{0,8},{4,12},{8,0},{12,4},{16,24},{20,28},{24,16},{28,20},{1,9},{5... | collective-permute-start | bytes 1572872 | tf_op jit(solution)/shard_map/ppermute | solution.py:11
  617.5 13.1 %collective-permute-start.17 = (f32[2,1,32,2048]{3,2,1,0:T(8,128)S(1)}, f32[2,1,32,2048]{3,2,1,0:T(8,128)S(1)}, u32[]{:S(2)}, u32[]{:S(2)}) collective-permute-start(f32[2,1,32,2048]{3,2,1,0:T(8,128)S(1)} %collective-permute-done.16), channel_id=1, source_target_pairs={{0,16},{4,20},{8,24},{12,28},{16,0},{20,4},{24,8},{28,12},{1,17},{... | collective-permute-start | bytes 1572872 | tf_op jit(solution)/shard_map/ppermute | solution.py:11
  630.6 12.3 %collective-permute-start.18 = (f32[2,1,32,2048]{3,2,1,0:T(8,128)S(1)}, f32[2,1,32,2048]{3,2,1,0:T(8,128)S(1)}, u32[]{:S(2)}, u32[]{:S(2)}) collective-permute-start(f32[2,1,32,2048]{3,2,1,0:T(8,128)S(1)} %collective-permute-done.17), channel_id=1, source_target_pairs={{0,1},{1,0},{2,3},{3,2},{4,5},{5,4},{6,7},{7,6},{8,9},{9,8},{10,11... | collective-permute-start | bytes 1572872 | tf_op jit(solution)/shard_map/ppermute | solution.py:11
  642.9 23.5 %collective-permute-start.19 = (f32[2,1,32,2048]{3,2,1,0:T(8,128)S(1)}, f32[2,1,32,2048]{3,2,1,0:T(8,128)S(1)}, u32[]{:S(2)}, u32[]{:S(2)}) collective-permute-start(f32[2,1,32,2048]{3,2,1,0:T(8,128)S(1)} %collective-permute-done.18), channel_id=1, source_target_pairs={{0,2},{1,3},{2,0},{3,1},{4,6},{5,7},{6,4},{7,5},{8,10},{9,11},{10,... | collective-permute-start | bytes 1572872 | tf_op jit(solution)/shard_map/ppermute | solution.py:11
  719.5 1.8 copy-start.6
  725.4 91.7 %all-reduce.24.cloned.1.call-start = ((), (), s32[]{:S(2)}) async-start(), calls=%async_computation.7 | async-start | bytes 262144 | tf_op jit(solution)/shard_map/psum | solution.py:37
  817.1 2.9 copy-start.7
  817.1 2.9 copy-start.11
  825.8 2.0 collective-permute-start.20
  827.7 14.0 %collective-permute-start.21 = (f32[2,1,32,2048]{3,2,1,0:T(8,128)S(1)}, f32[2,1,32,2048]{3,2,1,0:T(8,128)S(1)}, u32[]{:S(2)}, u32[]{:S(2)}) collective-permute-start(f32[2,1,32,2048]{3,2,1,0:T(8,128)S(1)} %collective-permute-done.20), channel_id=1, source_target_pairs={{0,8},{4,12},{8,0},{12,4},{16,24},{20,28},{24,16},{28,20},{1,9},{5... | collective-permute-start | bytes 1572872 | tf_op jit(solution)/shard_map/ppermute | solution.py:11
  841.7 13.1 %collective-permute-start.22 = (f32[2,1,32,2048]{3,2,1,0:T(8,128)S(1)}, f32[2,1,32,2048]{3,2,1,0:T(8,128)S(1)}, u32[]{:S(2)}, u32[]{:S(2)}) collective-permute-start(f32[2,1,32,2048]{3,2,1,0:T(8,128)S(1)} %collective-permute-done.21), channel_id=1, source_target_pairs={{0,16},{4,20},{8,24},{12,28},{16,0},{20,4},{24,8},{28,12},{1,17},{... | collective-permute-start | bytes 1572872 | tf_op jit(solution)/shard_map/ppermute | solution.py:11
  854.8 12.3 %collective-permute-start.23 = (f32[2,1,32,2048]{3,2,1,0:T(8,128)S(1)}, f32[2,1,32,2048]{3,2,1,0:T(8,128)S(1)}, u32[]{:S(2)}, u32[]{:S(2)}) collective-permute-start(f32[2,1,32,2048]{3,2,1,0:T(8,128)S(1)} %collective-permute-done.22), channel_id=1, source_target_pairs={{0,1},{1,0},{2,3},{3,2},{4,5},{5,4},{6,7},{7,6},{8,9},{9,8},{10,11... | collective-permute-start | bytes 1572872 | tf_op jit(solution)/shard_map/ppermute | solution.py:11
  867.1 23.5 %collective-permute-start.24 = (f32[2,1,32,2048]{3,2,1,0:T(8,128)S(1)}, f32[2,1,32,2048]{3,2,1,0:T(8,128)S(1)}, u32[]{:S(2)}, u32[]{:S(2)}) collective-permute-start(f32[2,1,32,2048]{3,2,1,0:T(8,128)S(1)} %collective-permute-done.23), channel_id=1, source_target_pairs={{0,2},{1,3},{2,0},{3,1},{4,6},{5,7},{6,4},{7,5},{8,10},{9,11},{10,... | collective-permute-start | bytes 1572872 | tf_op jit(solution)/shard_map/ppermute | solution.py:11
  939.3 15.1 %collective-permute-start.26 = (f32[1,32,32,1]{3,1,2,0:T(8,128)S(1)}, f32[1,32,32,1]{3,1,2,0:T(8,128)S(1)}, u32[]{:S(2)}, u32[]{:S(2)}) collective-permute-start(f32[1,32,32,1]{3,1,2,0:T(8,128)S(1)} %bitcast.338), channel_id=1, source_target_pairs={{1,0},{2,1},{3,2},{5,4},{6,5},{7,6},{9,8},{10,9},{11,10},{13,12},{... | collective-permute-start | bytes 12296 | tf_op jit(solution)/shard_map/ppermute | solution.py:17
  941.7 14.7 %collective-permute-start.25 = (f32[1,32,1,64]{3,1,2,0:T(8,128)S(1)}, f32[1,32,1,64]{3,1,2,0:T(8,128)S(1)}, u32[]{:S(2)}, u32[]{:S(2)}) collective-permute-start(f32[1,32,1,64]{3,1,2,0:T(8,128)S(1)} %slice.232), channel_id=1, source_target_pairs={{4,0},{8,4},{12,8},{16,12},{20,16},{24,20},{28,24},{5,1},{9,5},{13... | collective-permute-start | bytes 24584 | tf_op jit(solution)/shard_map/ppermute | solution.py:17
Sparse Core Ops, SparseCore 0:
  53.9 35.1 all-reduce.9
  92.1 53.1 all-reduce.11
  277.6 35.3 all-reduce.13
  315.9 53.1 all-reduce.15
  501.5 35.3 all-reduce.17
  539.8 53.1 all-reduce.19
  725.5 35.3 all-reduce.21
  763.9 53.1 all-reduce.23
